TPU v7x, 256 devices: a whole 4x4x8 slice. The times are simulated.
256 devices in a mesh: comp: 2 (over core), space: 64 (over x, y_hi, z), trc: 2 (over y_lo).
Axes of the slice: x: 4, y: 4 (y_hi: 2, y_lo: 2; y = y_hi * 2 + y_lo), z: 8, core: 2. Of those that a mesh axis runs over, the one named last changes fastest.
Arguments:
- tracers: float32 [16, 8, 512, 1024], P(('comp', 'trc'), None, 'space'), may hold values from -6 to 6
- flow: float32 [16, 512, 1024], P(('comp', 'trc'), 'space'), may hold values from -4 to 4
- reaction_rates: float32 [16, 16], replicated, may hold values from -1.5 to 1.5
- land_mask: int32 [512, 1024], P('space'), may hold values 0 or 1
- layers: int32 [512, 1024], P('space'), may hold values from 1 to 8
Outputs:
- tracers_out: float32 [16, 8, 512, 1024], P(('comp', 'trc'), None, 'space')
- flow_out: float32 [16, 512, 1024], P(('comp', 'trc'), 'space')
All inputs are finite; a program needn't handle non-finite values. No bound on the sum of `land_mask` on one device may be relied on, other than what follows from the above.
Results may differ from a plain program's by a relative error of at most 0.0003.
Values sent between devices are 32-bit elements; how exact they have to be, the bound alone decides.
A program may use at most 64 MiB of HBM per device.

v0:
```python
import functools

import jax
import jax.numpy as jnp
from jax import lax
from jax.experimental import pallas as pl
from jax.experimental.pallas import tpu as pltpu
from jax.sharding import PartitionSpec as P

STEPS = 2
COURANT = 0.25
VISCOSITY = 0.2
CORIOLIS = 0.3
FRICTION = 0.1
DIFFUSION = 0.3
REACT_STEP = 0.5

MESH = pl.DeviceIdType.MESH
F32 = jnp.float32
ROWS = 8
DEEP = 24
GHOST = 4
SPAN = ROWS + 2 * GHOST
PAIR = 256


def limited(before, after):
    return jnp.maximum(jnp.minimum(after, 0.0), jnp.minimum(before, jnp.maximum(after, 0.0)))


def roll_lanes(a, by):
    return pltpu.roll(a, by % a.shape[-1], a.ndim - 1)


def kernel(
    tracers, flow, land, layers, matrix, out, flow_out,
    tr_v, fl_v, dep_v, stage, grid, first, part, second, coef_x, coef_y, mix_w, natural,
    field, depth_v, packed, ext, final, velocity_send,
    in_local, in_sem_s, in_sem_r, fl_local, fl_sem_s, fl_sem_r, dep_s, dep_r,
    halo_s, halo_r, mix_s, mix_r, out_s, out_r, own_out, fo_s, fo_r, fo_own,
):
    ny = tracers.shape[-1]
    c = lax.axis_index("comp")
    sp = lax.axis_index("space")
    t = lax.axis_index("trc")
    n = lax.axis_size("space")
    v = 2 * t + c
    w = 2 * c + t
    has_prev = sp > 0
    has_next = sp < n - 1

    def at(cc, ss, tt):
        return {"comp": cc, "space": ss, "trc": tt}

    def remote(src, dst, s, r, dev):
        return pltpu.make_async_remote_copy(
            src_ref=src, dst_ref=dst, send_sem=s, recv_sem=r, device_id=dev, device_id_type=MESH
        )

    my_flow = pltpu.make_async_copy(
        flow.at[pl.ds(2 * c, 2)], field.at[0, c, :, pl.ds(ROWS, ROWS)], fl_local.at[0]
    )
    all_flow = pltpu.make_async_copy(flow, fl_v, fl_local.at[1])
    all_tr = pltpu.make_async_copy(tracers, tr_v, in_local.at[0])
    own_tr = [
        pltpu.make_async_copy(tracers.at[:, 2 * v + e], stage.at[w, e], in_local.at[1 + e])
        for e in range(2)
    ]
    all_tr.start()
    all_flow.start()
    my_flow.start()
    for copy in own_tr:
        copy.start()

    barrier = pltpu.get_barrier_semaphore()
    peers = [(c, 1 - t), (1 - c, 1 - t), (1 - c, t)]
    for cc, tt in peers:
        pl.semaphore_signal(barrier, inc=1, device_id=at(cc, sp, tt), device_id_type=MESH)

    @pl.when(has_prev)
    def _():
        for cc in range(2):
            pl.semaphore_signal(barrier, inc=1, device_id=at(cc, sp - 1, t), device_id_type=MESH)

    @pl.when(has_next)
    def _():
        for cc in range(2):
            pl.semaphore_signal(barrier, inc=1, device_id=at(cc, sp + 1, t), device_id_type=MESH)

    dep_v[...] = jnp.where(land[...] > 0, layers[...], 0).astype(F32)
    depth_v[ROWS : 2 * ROWS] = dep_v[...]

    @pl.when(jnp.logical_not(has_prev))
    def _():
        depth_v[0:ROWS] = jnp.zeros((ROWS, ny), F32)
        for comp in range(2):
            for e in range(2):
                field[0, comp, e, 0:ROWS] = jnp.zeros((ROWS, ny), F32)
        for step in range(2):
            for slot in range(4):
                for row in range(GHOST):
                    grid[step, slot, row] = jnp.zeros((8, ny), F32)

    @pl.when(jnp.logical_not(has_next))
    def _():
        depth_v[2 * ROWS :] = jnp.zeros((ROWS, ny), F32)
        for comp in range(2):
            for e in range(2):
                field[0, comp, e, 2 * ROWS :] = jnp.zeros((ROWS, ny), F32)
        for step in range(2):
            for slot in range(4):
                for row in range(GHOST):
                    grid[step, slot, GHOST + ROWS + row] = jnp.zeros((8, ny), F32)

    @pl.when(v == 0)
    def _():
        for step in range(2):
            for p in range(2):
                ext[step, 0, p] = jnp.zeros((ROWS, 8, ny), F32)

    @pl.when(v == 3)
    def _():
        for step in range(2):
            for p in range(2):
                ext[step, 1, p] = jnp.zeros((ROWS, 8, ny), F32)

    pl.semaphore_wait(
        barrier, 3 + 2 * jnp.where(has_prev, 1, 0) + 2 * jnp.where(has_next, 1, 0)
    )

    def in_copy(k, e):
        cc, tt = peers[k]
        return remote(
            tr_v.at[:, 2 * (2 * tt + cc) + e], stage.at[w, e],
            in_sem_s.at[k, e], in_sem_r.at[w, e], at(cc, sp, tt),
        )

    all_tr.wait()
    for k in (2, 0, 1):
        for e in range(2):
            in_copy(k, e).start()

    def flow_copy(d, cc):
        return remote(
            fl_v.at[pl.ds(2 * cc, 2)],
            field.at[0, c, :, pl.ds(ROWS * (1 - d), ROWS)],
            fl_sem_s.at[d + 1, cc], fl_sem_r.at[1 - d, c], at(cc, sp + d, t),
        )

    def dep_copy(d):
        return remote(
            dep_v, depth_v.at[pl.ds(ROWS * (1 - d), ROWS)],
            dep_s.at[d + 1], dep_r.at[1 - d], at(c, sp + d, t),
        )

    partner_flow = remote(
        fl_v.at[pl.ds(2 * (1 - c), 2)], field.at[0, c, :, pl.ds(ROWS, ROWS)],
        fl_sem_s.at[1, 0], fl_sem_r.at[1, 0], at(1 - c, sp, t),
    )
    all_flow.wait()
    partner_flow.start()

    @pl.when(has_prev)
    def _():
        dep_copy(-1).start()
        for cc in range(2):
            flow_copy(-1, cc).start()

    @pl.when(has_next)
    def _():
        dep_copy(1).start()
        for cc in range(2):
            flow_copy(1, cc).start()

    def halo_copy(step, slot, d):
        low = d < 0
        return remote(
            grid.at[step, slot, pl.ds(GHOST if low else ROWS, GHOST)],
            grid.at[step, slot, pl.ds(GHOST + ROWS if low else 0, GHOST)],
            halo_s.at[step, slot, 0 if low else 1], halo_r.at[step, slot, 1 if low else 0],
            at(c, sp + d, t),
        )

    def halo_start(step, slot):
        @pl.when(has_prev)
        def _():
            halo_copy(step, slot, -1).start()

        @pl.when(has_next)
        def _():
            halo_copy(step, slot, 1).start()

    def halo_wait(step, slot):
        @pl.when(has_prev)
        def _():
            halo_copy(step, slot, 1).wait_recv()

        @pl.when(has_next)
        def _():
            halo_copy(step, slot, -1).wait_recv()

    def halo_sent(step, slot):
        @pl.when(has_prev)
        def _():
            halo_copy(step, slot, -1).wait_send()

        @pl.when(has_next)
        def _():
            halo_copy(step, slot, 1).wait_send()

    def regroup(slot):
        def tile(q, _):
            lanes = pl.ds(pl.multiple_of(q * 128, 128), 128)
            x = stage[slot, :, :, :, lanes].reshape(8, ROWS, 128)
            grid[0, slot, pl.ds(GHOST, ROWS), :, lanes] = jnp.swapaxes(x, 0, 1)
            return 0

        lax.fori_loop(0, ny // 128, tile, 0)

    def arrived(k):
        cc, tt = peers[k]
        slot = 2 * cc + tt
        for e in range(2):
            remote(
                stage.at[slot, e], stage.at[slot, e], in_sem_s.at[k, e], in_sem_r.at[slot, e],
                at(cc, sp, tt),
            ).wait_recv()
        regroup(slot)
        halo_start(0, slot)

    for copy in own_tr:
        copy.wait()
    regroup(w)
    halo_start(0, w)
    arrived(2)

    my_flow.wait()
    partner_flow.wait_recv()

    @pl.when(has_prev)
    def _():
        dep_copy(1).wait_recv()
        for cc in range(2):
            remote(
                fl_v.at[pl.ds(0, 2)], field.at[0, cc, :, pl.ds(0, ROWS)],
                fl_sem_s.at[0, cc], fl_sem_r.at[0, cc], at(cc, sp - 1, t),
            ).wait_recv()

    @pl.when(has_next)
    def _():
        dep_copy(-1).wait_recv()
        for cc in range(2):
            remote(
                fl_v.at[pl.ds(0, 2)], field.at[0, cc, :, pl.ds(2 * ROWS, ROWS)],
                fl_sem_s.at[2, cc], fl_sem_r.at[2, cc], at(cc, sp + 1, t),
            ).wait_recv()

    lane_deep = lax.broadcasted_iota(jnp.int32, (DEEP, ny), 1)
    top_half = lax.broadcasted_iota(jnp.int32, (8, ny), 0) < 4
    lane = lax.broadcasted_iota(jnp.int32, (8, ny), 1)
    at_first = lane == 0
    at_last = lane == ny - 1

    def wet_of(level, rows):
        return jnp.where(depth_v[rows] > level.astype(F32), 1.0, 0.0)

    def lap(a):
        left = jnp.where(lane_deep == 0, 0.0, roll_lanes(a, 1))
        right = jnp.where(lane_deep == ny - 1, 0.0, roll_lanes(a, -1))
        return pltpu.roll(a, 1, 0) + pltpu.roll(a, DEEP - 1, 0) + left + right - 4.0 * a

    def put_coefs(e, base, face):
        up = jnp.maximum(face, 0.0)
        down = jnp.minimum(face, 0.0)
        natural[e, base] = -COURANT * up
        natural[e, base + 1] = (-COURANT * 0.5) * up * (1.0 - COURANT * up)
        natural[e, base + 2] = -COURANT * down
        natural[e, base + 3] = (COURANT * 0.5) * down * (1.0 + COURANT * down)

    def spread_rows(ref, k, j):
        one = jnp.broadcast_to(ref[0, k, j : j + 1, :], (8, ny))
        two = jnp.broadcast_to(ref[1, k, j : j + 1, :], (8, ny))
        return jnp.where(top_half, one, two)

    def velocities(step, _):
        def level(e, _):
            wet = wet_of(2 * v + e, slice(None))
            u = field[step, 0, e]
            r = field[step, 1, e]
            u_new = wet * (u + CORIOLIS * r + VISCOSITY * lap(u) - FRICTION * u)
            r_new = wet * (r - CORIOLIS * u + VISCOSITY * lap(r) - FRICTION * r)
            field[step + 1, 0, e] = u_new
            field[step + 1, 1, e] = r_new
            face = 0.5 * (u_new + pltpu.roll(u_new, DEEP - 1, 0)) * wet * pltpu.roll(wet, DEEP - 1, 0)
            put_coefs(e, 0, face)
            wet_right = jnp.where(lane_deep == ny - 1, 0.0, roll_lanes(wet, -1))
            face = 0.5 * (r_new + roll_lanes(r_new, -1)) * wet * wet_right
            put_coefs(e, 4, face)
            return 0

        lax.fori_loop(0, 2, level, 0)
        shift = ROWS - GHOST
        for i in range(1, 14):
            for k in range(4):
                coef_x[step, i - 1, k] = spread_rows(natural, k, i + shift)
        for i in range(2, 14):
            for k in range(4):
                coef_y[step, i - 2, k] = spread_rows(natural, 4 + k, i + shift)
        return 0

    lax.fori_loop(0, STEPS, velocities, 0)

    middle = slice(ROWS, 2 * ROWS)
    above = jnp.where(v > 0, DIFFUSION, 0.0).astype(F32)
    wet_a = wet_of(2 * v, middle)
    wet_b = wet_of(2 * v + 1, middle)
    natural[0, 0, 0:ROWS] = DIFFUSION * wet_a * wet_b
    natural[1, 0, 0:ROWS] = DIFFUSION * wet_a * wet_b
    natural[0, 1, 0:ROWS] = above * wet_a * wet_of(2 * v - 1, middle)
    natural[1, 1, 0:ROWS] = DIFFUSION * wet_b * wet_of(2 * v + 2, middle)
    for row in range(ROWS):
        for k in range(2):
            mix_w[row, k] = spread_rows(natural, k, row)

    for e in range(2):
        velocity_send[0, e] = field[STEPS, c, e, ROWS : 2 * ROWS]
        velocity_send[1, e] = field[STEPS, 1 - c, e, ROWS : 2 * ROWS]
    flow_own = pltpu.make_async_copy(velocity_send.at[0], flow_out.at[pl.ds(2 * c, 2)], fo_own.at[0])
    flow_far = remote(
        velocity_send.at[1], flow_out.at[pl.ds(2 * c, 2)], fo_s.at[0], fo_r.at[0], at(1 - c, sp, t)
    )
    flow_own.start()
    flow_far.start()

    def along_x(step, load, first_face, last_face, put):
        def chunk(q, _):
            lanes = pl.ds(pl.multiple_of(q * PAIR, PAIR), PAIR)
            before = load(first_face - 1, lanes)
            here = load(first_face, lanes)
            ahead = load(first_face + 1, lanes)
            jump = ahead - here
            slope = limited(here - before, jump)
            last_flux = None
            for i in range(first_face, last_face + 1):
                far = load(i + 2, lanes)
                next_jump = far - ahead
                next_slope = limited(jump, next_jump)
                k = i - 1
                flux = (
                    coef_x[step, k, 0, :, lanes] * here
                    + coef_x[step, k, 1, :, lanes] * slope
                    + coef_x[step, k, 2, :, lanes] * ahead
                    + coef_x[step, k, 3, :, lanes] * next_slope
                )
                if last_flux is not None:
                    put(i, lanes, here, flux - last_flux)
                last_flux = flux
                here, ahead, jump, slope = ahead, far, next_jump, next_slope
            return 0

        lax.fori_loop(0, ny // PAIR, chunk, 0)

    def along_y(step, i, a):
        right = jnp.where(at_last, 0.0, roll_lanes(a, -1))
        jump = right - a
        slope = limited(jnp.where(at_first, a, roll_lanes(jump, 1)), jump)
        flux = (
            coef_y[step, i - 2, 0] * a
            + coef_y[step, i - 2, 1] * slope
            + coef_y[step, i - 2, 2] * right
            + coef_y[step, i - 2, 3] * roll_lanes(slope, -1)
        )
        return flux - roll_lanes(flux, 1)

    def advance(step, slot):
        def put_one(i, lanes, here, change):
            part[i, :, lanes] = here + change

        along_x(step, lambda i, lanes: grid[step, slot, i, :, lanes], 1, 13, put_one)

        def row_one(i, _):
            first[i] = part[i] + along_y(step, i, grid[step, slot, i])
            return 0

        lax.fori_loop(2, 14, row_one, 0)

        def put_two(i, lanes, here, change):
            part[i, :, lanes] = (grid[step, slot, i, :, lanes] + here) + change

        along_x(step, lambda i, lanes: first[i, :, lanes], 3, 11, put_two)

        def row_two(i, _):
            second[slot, i - GHOST] = 0.5 * (part[i] + along_y(step, i, first[i]))
            return 0

        lax.fori_loop(GHOST, GHOST + ROWS, row_two, 0)

    def swap_halves(a):
        return pltpu.roll(a, 4, 0)

    def mix_copy(step, p, d):
        up = v + d
        return remote(
            packed.at[step, p, 0 if d < 0 else 1], ext.at[step, 1 if d < 0 else 0, p],
            mix_s.at[step, p, 0 if d < 0 else 1], mix_r.at[step, p, 1 if d < 0 else 0],
            at(lax.rem(up, 2), sp, up // 2),
        )

    def mix_start(step, p):
        def row(i, _):
            a = second[p, i]
            b = second[p + 2, i]
            packed[step, p, 0, i] = jnp.where(top_half, a, swap_halves(b))
            packed[step, p, 1, i] = jnp.where(top_half, swap_halves(a), b)
            return 0

        lax.fori_loop(0, ROWS, row, 0)

        @pl.when(v > 0)
        def _():
            mix_copy(step, p, -1).start()

        @pl.when(v < 3)
        def _():
            mix_copy(step, p, 1).start()

    def mix_wait(step, p):
        @pl.when(v > 0)
        def _():
            mix_copy(step, p, 1).wait_recv()

        @pl.when(v < 3)
        def _():
            mix_copy(step, p, -1).wait_recv()

    def mix_sent(step, p):
        @pl.when(v > 0)
        def _():
            mix_copy(step, p, -1).wait_send()

        @pl.when(v < 3)
        def _():
            mix_copy(step, p, 1).wait_send()

    def settle(step, put, rows):
        def row(i, _):
            inner = mix_w[i, 0]
            outer = mix_w[i, 1]
            mixed = [None] * 4
            for p in range(2):
                low = ext[step, 0, p, i]
                high = ext[step, 1, p, i]
                beyond = (
                    jnp.where(top_half, low, swap_halves(high)),
                    jnp.where(top_half, swap_halves(low), high),
                )
                for half in range(2):
                    a = second[p + 2 * half, i]
                    mixed[p + 2 * half] = (
                        a + inner * (swap_halves(a) - a) + outer * (beyond[half] - a)
                    )
            whole = jnp.concatenate(mixed, axis=0)
            soft = whole / (1.0 + jnp.abs(whole))
            done = whole + jnp.dot(
                matrix[...], soft, precision=lax.Precision.HIGHEST, preferred_element_type=F32
            )
            for slot in range(4):
                put(slot, i, done[8 * slot : 8 * slot + 8])
            return 0

        lax.fori_loop(*rows, row, 0)

    def run(step, order):
        own_pair, far_pair = t, 1 - t
        for number, slot in enumerate(order):
            if step == 0 and number >= 2:
                arrived(number - 2)
            halo_wait(step, slot)
            advance(step, slot)
            if number == 1:
                mix_start(step, own_pair)
        mix_start(step, far_pair)
        for p in range(2):
            mix_wait(step, p)

    order = [w, 2 * (1 - c) + t, 2 * c + 1 - t, 2 * (1 - c) + 1 - t]
    run(0, order)

    def put_next(slot, i, a):
        grid[1, slot, GHOST + i] = a

    settle(0, put_next, (0, ROWS))
    for slot in order:
        halo_start(1, slot)
    run(1, order)

    def put_final(slot, i, a):
        final[slot, i] = a

    half = ROWS // 2

    def out_copy(k, h):
        cc, tt = peers[k]
        return remote(
            final.at[2 * cc + tt, pl.ds(half * h, half)], out.at[v, pl.ds(half * h, half)],
            out_s.at[k, h], out_r.at[v, h], at(cc, sp, tt),
        )

    own_copies = []
    for h in range(2):
        settle(1, put_final, (half * h, half * (h + 1)))
        for k in (0, 1, 2):
            out_copy(k, h).start()
        copy = pltpu.make_async_copy(
            final.at[w, pl.ds(half * h, half)], out.at[v, pl.ds(half * h, half)], own_out.at[h]
        )
        copy.start()
        own_copies.append(copy)

    for copy in own_copies:
        copy.wait()
    flow_own.wait()
    flow_far.wait_send()
    remote(
        velocity_send.at[1], flow_out.at[pl.ds(2 * (1 - c), 2)], fo_s.at[0], fo_r.at[0],
        at(1 - c, sp, t),
    ).wait_recv()
    for k in range(3):
        for e in range(2):
            in_copy(k, e).wait_send()
    partner_flow.wait_send()

    @pl.when(has_prev)
    def _():
        dep_copy(-1).wait_send()
        for cc in range(2):
            flow_copy(-1, cc).wait_send()

    @pl.when(has_next)
    def _():
        dep_copy(1).wait_send()
        for cc in range(2):
            flow_copy(1, cc).wait_send()

    for step in range(STEPS):
        for slot in range(4):
            halo_sent(step, slot)
        for p in range(2):
            mix_sent(step, p)
    for k in range(3):
        cc, tt = peers[k]
        source = 2 * tt + cc
        for h in range(2):
            out_copy(k, h).wait_send()
            remote(
                final.at[w, pl.ds(half * h, half)], out.at[source, pl.ds(half * h, half)],
                out_s.at[k, h], out_r.at[source, h], at(cc, sp, tt),
            ).wait_recv()


def place(blocks, flow, out, flow_out):
    x = jnp.swapaxes(blocks[0], 0, 1)
    for e in range(2):
        for s in range(4):
            out[s, e] = x[4 * e + s]

    @pl.when(pl.program_id(0) == 0)
    def _():
        flow_out[...] = flow[...]


def body(tracers, flow, reaction_rates, land_mask, layers):
    ny = tracers.shape[-1]
    rates = REACT_STEP * reaction_rates.reshape(4, 1, 4, 4, 1, 4)
    matrix = (rates * jnp.eye(2, dtype=F32).reshape(1, 2, 1, 1, 2, 1)).reshape(32, 32)
    vmem = pl.BlockSpec(memory_space=pltpu.VMEM)
    anywhere = pl.BlockSpec(memory_space=pl.ANY)
    dma = pltpu.SemaphoreType.DMA
    blocks, flow_done = pl.pallas_call(
        kernel,
        out_shape=(
            jax.ShapeDtypeStruct((4, ROWS, 8, ny), F32),
            jax.ShapeDtypeStruct((4, ROWS, ny), F32),
        ),
        in_specs=[anywhere, anywhere, vmem, vmem, vmem],
        out_specs=(anywhere, anywhere),
        scratch_shapes=[
            pltpu.VMEM((4, 8, ROWS, ny), F32),
            pltpu.VMEM((4, ROWS, ny), F32),
            pltpu.VMEM((ROWS, ny), F32),
            pltpu.VMEM((4, 2, 4, ROWS, ny), F32),
            pltpu.VMEM((STEPS, 4, SPAN, 8, ny), F32),
            pltpu.VMEM((SPAN, 8, ny), F32),
            pltpu.VMEM((SPAN, 8, ny), F32),
            pltpu.VMEM((4, ROWS, 8, ny), F32),
            pltpu.VMEM((STEPS, 13, 4, 8, ny), F32),
            pltpu.VMEM((STEPS, 12, 4, 8, ny), F32),
            pltpu.VMEM((ROWS, 2, 8, ny), F32),
            pltpu.VMEM((2, 8, DEEP, ny), F32),
            pltpu.VMEM((STEPS + 1, 2, 2, DEEP, ny), F32),
            pltpu.VMEM((DEEP, ny), F32),
            pltpu.VMEM((STEPS, 2, 2, ROWS, 8, ny), F32),
            pltpu.VMEM((STEPS, 2, 2, ROWS, 8, ny), F32),
            pltpu.VMEM((4, ROWS, 8, ny), F32),
            pltpu.VMEM((2, 2, ROWS, ny), F32),
            dma((3,)), dma((3, 2)), dma((4, 2)),
            dma((2,)), dma((3, 2)), dma((3, 2)), dma((3,)), dma((3,)),
            dma((STEPS, 4, 2)), dma((STEPS, 4, 2)),
            dma((STEPS, 2, 2)), dma((STEPS, 2, 2)),
            dma((3, 2)), dma((4, 2)), dma((2,)),
            dma((1,)), dma((1,)), dma((1,)),
        ],
        compiler_params=pltpu.CompilerParams(
            collective_id=0, has_side_effects=True, vmem_limit_bytes=48 * 1024 * 1024
        ),
        name="ocean",
    )(tracers, flow, land_mask, layers, matrix)
    return pl.pallas_call(
        place,
        grid=(4,),
        out_shape=(
            jax.ShapeDtypeStruct(tracers.shape, F32),
            jax.ShapeDtypeStruct(flow.shape, F32),
        ),
        in_specs=[
            pl.BlockSpec((1, ROWS, 8, ny), lambda g: (g, 0, 0, 0)),
            pl.BlockSpec((4, ROWS, ny), lambda g: (0, 0, 0)),
        ],
        out_specs=(
            pl.BlockSpec((4, 2, ROWS, ny), lambda g: (0, g, 0, 0)),
            pl.BlockSpec((4, ROWS, ny), lambda g: (0, 0, 0)),
        ),
        name="place",
    )(blocks, flow_done)


def solution(mesh):
    placed = (
        P(("comp", "trc"), None, "space", None),
        P(("comp", "trc"), "space", None),
        P(),
        P("space", None),
        P("space", None),
    )
    return jax.shard_map(
        body,
        mesh=mesh,
        in_specs=placed,
        out_specs=(P(("comp", "trc"), None, "space", None), P(("comp", "trc"), "space", None)),
        check_vma=False,
    )
```

profile of v0, /device:TPU:7, one launch (start us, length us, event | category | flops | bytes accessed | tf_op | source)
XLA Modules:
  0.0 133.1 jit_solution(12519283822569781471)
XLA Ops:
  0.6 0.7 broadcast_multiply_fusion.1
  1.3 0.1 mul.33
  1.4 0.0 copy-start.2
  1.4 0.1 broadcast_multiply_fusion
  1.5 0.0 copy-start.4
  1.6 0.0 copy-start.5
  1.6 0.2 mul.37.matrix
  1.8 0.6 copy-done.2
  2.3 0.0 copy-done.4
  2.3 0.0 copy-done.5
  2.3 0.0 copy-start
  2.3 1.2 copy-done
  3.6 124.4 %ocean.1 = (f32[4,8,8,1024]{3,2,1,0:T(8,128)S(1)}, f32[4,8,1024]{2,1,0:T(8,128)S(1)}) custom-call(f32[4,8,8,1024]{3,2,1,0:T(8,128)S(1)} %copy-done, f32[4,8,1024]{2,1,0:T(8,128)S(1)} %copy-done.2, s32[8,1024]{1,0:T(8,128)S(1)} %copy-done.4, s32[8,1024]{1,0:T(8,128)S(1)} %copy-done.5, f32[32,32]{1,0:T(8,128)S(1)} %mul.37.matrix), custom_call_target="tpu_custom_call" | custom-call | tf_op jit(solution)/shard_map/ocean/pallas_call | solution.py:579
  128.0 0.0 copy-start.1
  128.0 1.0 copy-done.1
  128.9 0.0 copy-start.3
  128.9 0.7 copy-done.3
  129.6 3.5 %place.1 = (f32[4,8,8,1024]{3,2,1,0:T(8,128)}, f32[4,8,1024]{2,1,0:T(8,128)}) custom-call(f32[4,8,8,1024]{3,2,1,0:T(8,128)} %copy-done.1, f32[4,8,1024]{2,1,0:T(8,128)} %copy-done.3), custom_call_target="tpu_custom_call" | custom-call | tf_op jit(solution)/shard_map/place/pallas_call | solution.py:618
  (1 shorter events, 0.0 us)
Async XLA Ops:
  1.4 0.9 copy-start.2
  1.5 0.8 copy-start.4
  1.6 0.8 copy-start.5
  2.3 1.2 copy-start
  128.0 1.0 copy-start.1
  128.9 0.7 copy-start.3
where the time goes:
time: 134 us; the launch traced here: 133 us
  Pallas kernels  128 us (96%)
  local copies, waits for them, and re-layouts  3.7 us (3%)
    pallas_call x1, Pallas kernels, body(): pl.pallas_call(kernel, out_shape=(jax.ShapeDtypeStruct((4, ROWS, 8, ny),...  124 us
    pallas_call x1, Pallas kernels, body(): pl.pallas_call(place, grid=(4,), out_shape=(jax.ShapeDtypeStruct(tracers....  3.51 us
    unnamed x12, local copies, waits for them, and re-layouts  3.44 us

commit v1 on v0

v1 whole, which is shorter than its diff:
```python
import functools

import jax
import jax.numpy as jnp
from jax import lax
from jax.experimental import pallas as pl
from jax.experimental.pallas import tpu as pltpu
from jax.sharding import PartitionSpec as P

STEPS = 2
COURANT = 0.25
VISCOSITY = 0.2
CORIOLIS = 0.3
FRICTION = 0.1
DIFFUSION = 0.3
REACT_STEP = 0.5

MESH = pl.DeviceIdType.MESH
F32 = jnp.float32
ROWS = 8
DEEP = 24
GHOST = 4
SPAN = ROWS + 2 * GHOST
HALF = ROWS // 2
ALL_VMEM = 67_043_328
LINE = 8
PAIR = 256


def limited(before, after):
    return jnp.maximum(jnp.minimum(after, 0.0), jnp.minimum(before, jnp.maximum(after, 0.0)))


def roll_lanes(a, by):
    return pltpu.roll(a, by % a.shape[-1], a.ndim - 1)


def kernel(
    tracers, flow, rates, land, layers, out, flow_out,
    tr_v, fl_v, dep_v, matrix, stage, grid, first, part, second, coef_x, coef_y, mix_w, natural,
    field, depth_v, packed, ext, final, velocity_send,
    in_local, in_sem_s, in_sem_r, fl_local, fl_sem_s, fl_sem_r, rel_s, rel_r, dep_s, dep_r,
    halo_s, halo_r, mix_s, mix_r, out_s, out_r, own_out, fo_s, fo_r, fo_own,
):
    ny = tracers.shape[-1]
    c = lax.axis_index("comp")
    sp = lax.axis_index("space")
    t = lax.axis_index("trc")
    n = lax.axis_size("space")
    w = 2 * c + t
    has_prev = sp > 0
    has_next = sp < n - 1

    def odd(strip):
        return lax.rem(strip // LINE, 2)

    def flipped(bit, strip):
        return lax.rem(bit + odd(strip), 2)

    flip = odd(sp)
    tl = flipped(t, sp)
    v = 2 * tl + c

    def at(cc, ss, tt):
        return {"comp": cc, "space": ss, "trc": tt}

    def holder(pair, strip):
        return at(lax.rem(pair, 2), strip, flipped(pair // 2, strip))

    def remote(src, dst, s, r, dev):
        return pltpu.make_async_remote_copy(
            src_ref=src, dst_ref=dst, send_sem=s, recv_sem=r, device_id=dev, device_id_type=MESH
        )

    middle = pl.ds(ROWS, ROWS)

    all_flow = pltpu.make_async_copy(flow, fl_v, fl_local.at[1])
    all_tr = pltpu.make_async_copy(tracers, tr_v, in_local.at[0])
    own_tr = [
        pltpu.make_async_copy(tracers.at[:, 2 * v + e], stage.at[w, e], in_local.at[1 + e])
        for e in range(2)
    ]
    my_flow = pltpu.make_async_copy(
        flow.at[pl.ds(2 * c, 2)], field.at[0, c, :, middle], fl_local.at[0]
    )
    all_flow.start()
    all_tr.start()
    for copy in own_tr:
        copy.start()

    @pl.when(flip == 0)
    def _():
        my_flow.start()

    barrier = pltpu.get_barrier_semaphore()
    peers = [(c, 1 - t), (1 - c, 1 - t), (1 - c, t)]

    def pair_of(cc, tt):
        return 2 * flipped(tt, sp) + cc

    for cc, tt in peers:
        pl.semaphore_signal(barrier, inc=1, device_id=at(cc, sp, tt), device_id_type=MESH)

    @pl.when(has_prev)
    def _():
        pl.semaphore_signal(barrier, inc=1, device_id=holder(v, sp - 1), device_id_type=MESH)

    @pl.when(has_next)
    def _():
        pl.semaphore_signal(barrier, inc=1, device_id=holder(v, sp + 1), device_id_type=MESH)

    dep_v[...] = jnp.where(land[...] > 0, layers[...], 0).astype(F32)
    depth_v[middle] = dep_v[...]

    @pl.when(jnp.logical_not(has_prev))
    def _():
        depth_v[0:ROWS] = jnp.zeros((ROWS, ny), F32)
        for comp in range(2):
            for e in range(2):
                field[0, comp, e, 0:ROWS] = jnp.zeros((ROWS, ny), F32)
        for step in range(2):
            for slot in range(4):
                for row in range(GHOST):
                    grid[step, slot, row] = jnp.zeros((8, ny), F32)

    @pl.when(jnp.logical_not(has_next))
    def _():
        depth_v[2 * ROWS :] = jnp.zeros((ROWS, ny), F32)
        for comp in range(2):
            for e in range(2):
                field[0, comp, e, 2 * ROWS :] = jnp.zeros((ROWS, ny), F32)
        for step in range(2):
            for slot in range(4):
                for row in range(GHOST):
                    grid[step, slot, GHOST + ROWS + row] = jnp.zeros((8, ny), F32)

    @pl.when(v == 0)
    def _():
        for step in range(2):
            for slot in range(4):
                ext[step, 0, slot] = jnp.zeros((HALF, 8, ny), F32)

    @pl.when(v == 3)
    def _():
        for step in range(2):
            for slot in range(4):
                ext[step, 1, slot] = jnp.zeros((HALF, 8, ny), F32)

    lines = lax.broadcasted_iota(jnp.int32, (32, 16), 0)
    names = lax.broadcasted_iota(jnp.int32, (32, 16), 1)
    pick = jnp.where(4 * (lines // 8) + lax.rem(lines, 4) == names, 1.0, 0.0)
    wide = jnp.dot(pick, rates[...], precision=lax.Precision.HIGHEST, preferred_element_type=F32)
    wide = lax.dot_general(
        wide, pick, (((1,), (1,)), ((), ())),
        precision=lax.Precision.HIGHEST, preferred_element_type=F32,
    )
    line = lax.broadcasted_iota(jnp.int32, (32, 32), 0)
    other = lax.broadcasted_iota(jnp.int32, (32, 32), 1)
    same_level = lax.rem(line // 4, 2) == lax.rem(other // 4, 2)
    matrix[...] = jnp.where(same_level, REACT_STEP * wide, 0.0)

    all_flow.wait()
    pl.semaphore_wait(barrier, 3 + jnp.where(has_prev, 1, 0) + jnp.where(has_next, 1, 0))

    def flow_copy(cc):
        return remote(
            fl_v.at[pl.ds(2 * cc, 2)], field.at[0, c, :, middle],
            fl_sem_s.at[cc], fl_sem_r.at[c], holder(2 * t + cc, sp),
        )

    def flow_from(cc):
        return remote(
            fl_v.at[pl.ds(0, 2)], field.at[0, cc, :, middle],
            fl_sem_s.at[cc], fl_sem_r.at[cc], at(cc, sp, tl),
        )

    @pl.when(flip == 0)
    def _():
        flow_copy(1 - c).start()

    @pl.when(flip == 1)
    def _():
        for cc in range(2):
            flow_copy(cc).start()

    def in_copy(k, e):
        cc, tt = peers[k]
        return remote(
            tr_v.at[:, 2 * pair_of(cc, tt) + e], stage.at[w, e],
            in_sem_s.at[k, e], in_sem_r.at[w, e], at(cc, sp, tt),
        )

    all_tr.wait()
    for k in (2, 0, 1):
        for e in range(2):
            in_copy(k, e).start()

    def dep_copy(d):
        return remote(
            dep_v, depth_v.at[pl.ds(ROWS * (1 - d), ROWS)],
            dep_s.at[d + 1], dep_r.at[1 - d], holder(v, sp + d),
        )

    def relay_copy(d):
        return remote(
            field.at[0, :, :, middle], field.at[0, :, :, pl.ds(ROWS * (1 - d), ROWS)],
            rel_s.at[d + 1], rel_r.at[1 - d], holder(v, sp + d),
        )

    @pl.when(has_prev)
    def _():
        dep_copy(-1).start()

    @pl.when(has_next)
    def _():
        dep_copy(1).start()

    def halo_copy(step, slot, d):
        low = d < 0
        return remote(
            grid.at[step, slot, pl.ds(GHOST if low else ROWS, GHOST)],
            grid.at[step, slot, pl.ds(GHOST + ROWS if low else 0, GHOST)],
            halo_s.at[step, slot, 0 if low else 1], halo_r.at[step, slot, 1 if low else 0],
            holder(v, sp + d),
        )

    def halo_start(step, slot):
        @pl.when(has_prev)
        def _():
            halo_copy(step, slot, -1).start()

        @pl.when(has_next)
        def _():
            halo_copy(step, slot, 1).start()

    def halo_wait(step, slot):
        @pl.when(has_prev)
        def _():
            halo_copy(step, slot, 1).wait_recv()

        @pl.when(has_next)
        def _():
            halo_copy(step, slot, -1).wait_recv()

    def halo_sent(step, slot):
        @pl.when(has_prev)
        def _():
            halo_copy(step, slot, -1).wait_send()

        @pl.when(has_next)
        def _():
            halo_copy(step, slot, 1).wait_send()

    def regroup(slot):
        def tile(q, _):
            lanes = pl.ds(pl.multiple_of(q * 128, 128), 128)
            x = stage[slot, :, :, :, lanes].reshape(8, ROWS, 128)
            grid[0, slot, pl.ds(GHOST, ROWS), :, lanes] = jnp.swapaxes(x, 0, 1)
            return 0

        lax.fori_loop(0, ny // 128, tile, 0, unroll=2)

    def arrived(k):
        cc, tt = peers[k]
        slot = 2 * cc + tt
        for e in range(2):
            remote(
                stage.at[slot, e], stage.at[slot, e], in_sem_s.at[k, e], in_sem_r.at[slot, e],
                at(cc, sp, tt),
            ).wait_recv()
        regroup(slot)
        halo_start(0, slot)

    for copy in own_tr:
        copy.wait()
    regroup(w)

    @pl.when(flip == 0)
    def _():
        my_flow.wait()
        flow_from(1 - c).wait_recv()

    @pl.when(flip == 1)
    def _():
        for cc in range(2):
            flow_from(cc).wait_recv()

    @pl.when(has_prev)
    def _():
        relay_copy(-1).start()

    @pl.when(has_next)
    def _():
        relay_copy(1).start()

    halo_start(0, w)
    arrived(2)

    @pl.when(has_prev)
    def _():
        dep_copy(1).wait_recv()
        relay_copy(1).wait_recv()

    @pl.when(has_next)
    def _():
        dep_copy(-1).wait_recv()
        relay_copy(-1).wait_recv()

    lane_deep = lax.broadcasted_iota(jnp.int32, (DEEP, ny), 1)
    top_half = lax.broadcasted_iota(jnp.int32, (8, ny), 0) < 4
    lane = lax.broadcasted_iota(jnp.int32, (8, ny), 1)
    at_first = lane == 0
    at_last = lane == ny - 1

    def wet_of(level, rows):
        return jnp.where(depth_v[rows] > level.astype(F32), 1.0, 0.0)

    def lap(a):
        left = jnp.where(lane_deep == 0, 0.0, roll_lanes(a, 1))
        right = jnp.where(lane_deep == ny - 1, 0.0, roll_lanes(a, -1))
        return pltpu.roll(a, 1, 0) + pltpu.roll(a, DEEP - 1, 0) + left + right - 4.0 * a

    def put_coefs(e, base, face):
        up = jnp.maximum(face, 0.0)
        down = jnp.minimum(face, 0.0)
        natural[e, base] = -COURANT * up
        natural[e, base + 1] = (-COURANT * 0.5) * up * (1.0 - COURANT * up)
        natural[e, base + 2] = -COURANT * down
        natural[e, base + 3] = (COURANT * 0.5) * down * (1.0 + COURANT * down)

    def spread_rows(ref, k, j):
        one = jnp.broadcast_to(ref[0, k, j : j + 1, :], (8, ny))
        two = jnp.broadcast_to(ref[1, k, j : j + 1, :], (8, ny))
        return jnp.where(top_half, one, two)

    def velocities(step, _):
        def level(e, _):
            wet = wet_of(2 * v + e, slice(None))
            u = field[step, 0, e]
            r = field[step, 1, e]
            u_new = wet * (u + CORIOLIS * r + VISCOSITY * lap(u) - FRICTION * u)
            r_new = wet * (r - CORIOLIS * u + VISCOSITY * lap(r) - FRICTION * r)
            field[step + 1, 0, e] = u_new
            field[step + 1, 1, e] = r_new
            face = 0.5 * (u_new + pltpu.roll(u_new, DEEP - 1, 0)) * wet * pltpu.roll(wet, DEEP - 1, 0)
            put_coefs(e, 0, face)
            wet_right = jnp.where(lane_deep == ny - 1, 0.0, roll_lanes(wet, -1))
            face = 0.5 * (r_new + roll_lanes(r_new, -1)) * wet * wet_right
            put_coefs(e, 4, face)
            return 0

        lax.fori_loop(0, 2, level, 0)
        shift = ROWS - GHOST
        for i in range(1, 14):
            for k in range(4):
                coef_x[step, i - 1, k] = spread_rows(natural, k, i + shift)
        for i in range(2, 14):
            for k in range(4):
                coef_y[step, i - 2, k] = spread_rows(natural, 4 + k, i + shift)
        return 0

    lax.fori_loop(0, STEPS, velocities, 0)

    own_rows = slice(ROWS, 2 * ROWS)
    above = jnp.where(v > 0, DIFFUSION, 0.0).astype(F32)
    wet_a = wet_of(2 * v, own_rows)
    wet_b = wet_of(2 * v + 1, own_rows)
    natural[0, 0, 0:ROWS] = DIFFUSION * wet_a * wet_b
    natural[1, 0, 0:ROWS] = DIFFUSION * wet_a * wet_b
    natural[0, 1, 0:ROWS] = above * wet_a * wet_of(2 * v - 1, own_rows)
    natural[1, 1, 0:ROWS] = DIFFUSION * wet_b * wet_of(2 * v + 2, own_rows)
    for row in range(ROWS):
        for k in range(2):
            mix_w[row, k] = spread_rows(natural, k, row)

    for comp in range(2):
        for e in range(2):
            velocity_send[comp, e] = field[STEPS, comp, e, own_rows]

    def velocity_copy(comp):
        return remote(
            velocity_send.at[comp], flow_out.at[pl.ds(2 * c, 2)],
            fo_s.at[comp], fo_r.at[c], at(comp, sp, tl),
        )

    def velocity_from(cc):
        return remote(
            velocity_send.at[0], flow_out.at[pl.ds(2 * cc, 2)],
            fo_s.at[0], fo_r.at[cc], holder(2 * t + cc, sp),
        )

    velocity_own = pltpu.make_async_copy(
        velocity_send.at[c], flow_out.at[pl.ds(2 * c, 2)], fo_own.at[0]
    )

    @pl.when(flip == 0)
    def _():
        velocity_own.start()
        velocity_copy(1 - c).start()

    @pl.when(flip == 1)
    def _():
        for comp in range(2):
            velocity_copy(comp).start()

    def along_x(step, load, first_face, last_face, put):
        def chunk(q, _):
            lanes = pl.ds(pl.multiple_of(q * PAIR, PAIR), PAIR)
            before = load(first_face - 1, lanes)
            here = load(first_face, lanes)
            ahead = load(first_face + 1, lanes)
            jump = ahead - here
            slope = limited(here - before, jump)
            last_flux = None
            for i in range(first_face, last_face + 1):
                far = load(i + 2, lanes)
                next_jump = far - ahead
                next_slope = limited(jump, next_jump)
                k = i - 1
                flux = (
                    coef_x[step, k, 0, :, lanes] * here
                    + coef_x[step, k, 1, :, lanes] * slope
                    + coef_x[step, k, 2, :, lanes] * ahead
                    + coef_x[step, k, 3, :, lanes] * next_slope
                )
                if last_flux is not None:
                    put(i, lanes, here, flux - last_flux)
                last_flux = flux
                here, ahead, jump, slope = ahead, far, next_jump, next_slope
            return 0

        lax.fori_loop(0, ny // PAIR, chunk, 0)

    def along_y(step, i, a):
        right = jnp.where(at_last, 0.0, roll_lanes(a, -1))
        jump = right - a
        slope = limited(jnp.where(at_first, a, roll_lanes(jump, 1)), jump)
        flux = (
            coef_y[step, i - 2, 0] * a
            + coef_y[step, i - 2, 1] * slope
            + coef_y[step, i - 2, 2] * right
            + coef_y[step, i - 2, 3] * roll_lanes(slope, -1)
        )
        return flux - roll_lanes(flux, 1)

    def advance(step, slot):
        def put_one(i, lanes, here, change):
            part[i, :, lanes] = here + change

        along_x(step, lambda i, lanes: grid[step, slot, i, :, lanes], 1, 13, put_one)

        def row_one(i, _):
            first[i] = part[i] + along_y(step, i, grid[step, slot, i])
            return 0

        lax.fori_loop(2, 14, row_one, 0, unroll=True)

        def put_two(i, lanes, here, change):
            part[i, :, lanes] = (grid[step, slot, i, :, lanes] + here) + change

        along_x(step, lambda i, lanes: first[i, :, lanes], 3, 11, put_two)

        def row_two(i, _):
            second[slot, i - GHOST] = 0.5 * (part[i] + along_y(step, i, first[i]))
            return 0

        lax.fori_loop(GHOST, GHOST + ROWS, row_two, 0, unroll=True)

    def swap_halves(a):
        return pltpu.roll(a, 4, 0)

    def mix_copy(step, slot, d):
        return remote(
            packed.at[step, slot, 0 if d < 0 else 1], ext.at[step, 1 if d < 0 else 0, slot],
            mix_s.at[step, slot, 0 if d < 0 else 1], mix_r.at[step, slot, 1 if d < 0 else 0],
            holder(v + d, sp),
        )

    def mix_start(step, slot):
        def row(i, _):
            a = second[slot, i]
            b = second[slot, i + HALF]
            packed[step, slot, 0, i] = jnp.where(top_half, a, swap_halves(b))
            packed[step, slot, 1, i] = jnp.where(top_half, swap_halves(a), b)
            return 0

        lax.fori_loop(0, HALF, row, 0, unroll=True)

        @pl.when(v > 0)
        def _():
            mix_copy(step, slot, -1).start()

        @pl.when(v < 3)
        def _():
            mix_copy(step, slot, 1).start()

    def mix_wait(step, slot):
        @pl.when(v > 0)
        def _():
            mix_copy(step, slot, 1).wait_recv()

        @pl.when(v < 3)
        def _():
            mix_copy(step, slot, -1).wait_recv()

    def mix_sent(step, slot):
        @pl.when(v > 0)
        def _():
            mix_copy(step, slot, -1).wait_send()

        @pl.when(v < 3)
        def _():
            mix_copy(step, slot, 1).wait_send()

    def settle(step, put, start, stop):
        def reacted(i, beyond_of):
            inner = mix_w[i, 0]
            outer = mix_w[i, 1]
            mixed = []
            for slot in range(4):
                a = second[slot, i]
                beyond = beyond_of(slot)
                mixed.append(a + inner * (swap_halves(a) - a) + outer * (beyond - a))
            whole = jnp.concatenate(mixed, axis=0)
            soft = whole / (1.0 + jnp.abs(whole))
            done = whole + jnp.dot(
                matrix[...], soft, precision=lax.Precision.HIGHEST, preferred_element_type=F32
            )
            for slot in range(4):
                put(slot, i, done[8 * slot : 8 * slot + 8])

        def rows(j, _):
            reacted(
                j,
                lambda slot: jnp.where(
                    top_half, ext[step, 0, slot, j], swap_halves(ext[step, 1, slot, j])
                ),
            )
            reacted(
                j + HALF,
                lambda slot: jnp.where(
                    top_half, swap_halves(ext[step, 0, slot, j]), ext[step, 1, slot, j]
                ),
            )
            return 0

        lax.fori_loop(start, stop, rows, 0)

    order = [w, 2 * (1 - c) + t, 2 * c + 1 - t, 2 * (1 - c) + 1 - t]

    between = jnp.logical_or(
        jnp.logical_and(has_prev, odd(sp - 1) != flip),
        jnp.logical_and(has_next, odd(sp + 1) != flip),
    )

    def run(step):
        if step == 0:

            @pl.when(between)
            def _():
                for number in range(2):
                    arrived(number)

        for number, slot in enumerate(order):
            halo_wait(step, slot)
            advance(step, slot)
            mix_start(step, slot)
            if step == 0 and number < 2:

                @pl.when(jnp.logical_not(between))
                def _(number=number):
                    arrived(number)
        for slot in order:
            mix_wait(step, slot)

    run(0)

    def put_next(slot, i, a):
        grid[1, slot, GHOST + i] = a

    settle(0, put_next, 0, HALF)
    for slot in order:
        halo_start(1, slot)
    run(1)

    def put_final(slot, i, a):
        final[slot, i] = a

    cuts = [(h, HALF * side + 2 * h) for h in range(2) for side in range(2)]

    def out_copy(k, part_of, row):
        cc, tt = peers[k]
        return remote(
            final.at[2 * cc + tt, pl.ds(row, 2)], out.at[v, pl.ds(row, 2)],
            out_s.at[k, part_of], out_r.at[v, part_of], at(cc, sp, tt),
        )

    def own_copy(part_of, row):
        return pltpu.make_async_copy(
            final.at[w, pl.ds(row, 2)], out.at[v, pl.ds(row, 2)], own_out.at[part_of]
        )

    for h in range(2):
        settle(1, put_final, 2 * h, 2 * h + 2)
        for part_of, (when, row) in enumerate(cuts):
            if when == h:
                for k in range(3):
                    out_copy(k, part_of, row).start()
                own_copy(part_of, row).start()

    for part_of, (_, row) in enumerate(cuts):
        own_copy(part_of, row).wait()

    @pl.when(flip == 0)
    def _():
        velocity_own.wait()
        velocity_copy(1 - c).wait_send()
        velocity_from(1 - c).wait_recv()
        flow_copy(1 - c).wait_send()

    @pl.when(flip == 1)
    def _():
        for cc in range(2):
            velocity_copy(cc).wait_send()
            velocity_from(cc).wait_recv()
            flow_copy(cc).wait_send()

    for k in range(3):
        for e in range(2):
            in_copy(k, e).wait_send()

    @pl.when(has_prev)
    def _():
        dep_copy(-1).wait_send()
        relay_copy(-1).wait_send()

    @pl.when(has_next)
    def _():
        dep_copy(1).wait_send()
        relay_copy(1).wait_send()

    for step in range(STEPS):
        for slot in range(4):
            halo_sent(step, slot)
            mix_sent(step, slot)
    for k in range(3):
        cc, tt = peers[k]
        source = pair_of(cc, tt)
        for part_of, (_, row) in enumerate(cuts):
            out_copy(k, part_of, row).wait_send()
            remote(
                final.at[w, pl.ds(row, 2)], out.at[source, pl.ds(row, 2)],
                out_s.at[k, part_of], out_r.at[source, part_of], at(cc, sp, tt),
            ).wait_recv()


def place(blocks, flow, out, flow_out, held, held_flow, ready, sems):
    ny = blocks.shape[-1]
    loads = [pltpu.make_async_copy(blocks.at[g], held.at[g], sems.at[5 + g]) for g in range(4)]
    for load in loads:
        load.start()
    flow_in = pltpu.make_async_copy(flow, held_flow, sems.at[9])
    flow_in.start()
    copies = []
    for pair in range(4):
        loads[pair].wait()

        def tile(q, _):
            lanes = pl.ds(pl.multiple_of(q * 128, 128), 128)
            x = jnp.swapaxes(held[pair, :, :, lanes], 0, 1)
            for e in range(2):
                for s in range(4):
                    ready[pair, s, e, :, lanes] = x[4 * e + s]
            return 0

        lax.fori_loop(0, ny // 128, tile, 0, unroll=4)
        copy = pltpu.make_async_copy(ready.at[pair], out.at[:, pl.ds(2 * pair, 2)], sems.at[pair])
        copy.start()
        copies.append(copy)
    flow_in.wait()
    flow_copy = pltpu.make_async_copy(held_flow, flow_out, sems.at[4])
    flow_copy.start()
    for copy in copies:
        copy.wait()
    flow_copy.wait()


def body(tracers, flow, reaction_rates, land_mask, layers):
    ny = tracers.shape[-1]
    vmem = pl.BlockSpec(memory_space=pltpu.VMEM)
    anywhere = pl.BlockSpec(memory_space=pl.ANY)
    dma = pltpu.SemaphoreType.DMA
    blocks, flow_done = pl.pallas_call(
        kernel,
        out_shape=(
            jax.ShapeDtypeStruct((4, ROWS, 8, ny), F32),
            jax.ShapeDtypeStruct((4, ROWS, ny), F32),
        ),
        in_specs=[pl.BlockSpec(memory_space=pltpu.HBM)] * 2 + [vmem] * 3,
        out_specs=(anywhere, anywhere),
        scratch_shapes=[
            pltpu.VMEM((4, 8, ROWS, ny), F32),
            pltpu.VMEM((4, ROWS, ny), F32),
            pltpu.VMEM((ROWS, ny), F32),
            pltpu.VMEM((32, 32), F32),
            pltpu.VMEM((4, 2, 4, ROWS, ny), F32),
            pltpu.VMEM((STEPS, 4, SPAN, 8, ny), F32),
            pltpu.VMEM((SPAN, 8, ny), F32),
            pltpu.VMEM((SPAN, 8, ny), F32),
            pltpu.VMEM((4, ROWS, 8, ny), F32),
            pltpu.VMEM((STEPS, 13, 4, 8, ny), F32),
            pltpu.VMEM((STEPS, 12, 4, 8, ny), F32),
            pltpu.VMEM((ROWS, 2, 8, ny), F32),
            pltpu.VMEM((2, 8, DEEP, ny), F32),
            pltpu.VMEM((STEPS + 1, 2, 2, DEEP, ny), F32),
            pltpu.VMEM((DEEP, ny), F32),
            pltpu.VMEM((STEPS, 4, 2, HALF, 8, ny), F32),
            pltpu.VMEM((STEPS, 2, 4, HALF, 8, ny), F32),
            pltpu.VMEM((4, ROWS, 8, ny), F32),
            pltpu.VMEM((2, 2, ROWS, ny), F32),
            dma((3,)), dma((3, 2)), dma((4, 2)),
            dma((2,)), dma((2,)), dma((2,)), dma((3,)), dma((3,)), dma((3,)), dma((3,)),
            dma((STEPS, 4, 2)), dma((STEPS, 4, 2)),
            dma((STEPS, 4, 2)), dma((STEPS, 4, 2)),
            dma((3, 4)), dma((4, 4)), dma((4,)),
            dma((2,)), dma((2,)), dma((1,)),
        ],
        compiler_params=pltpu.CompilerParams(
            collective_id=0, has_side_effects=True, vmem_limit_bytes=ALL_VMEM
        ),
        name="ocean",
    )(tracers, flow, reaction_rates, land_mask, layers)
    return pl.pallas_call(
        place,
        out_shape=(
            jax.ShapeDtypeStruct(tracers.shape, F32),
            jax.ShapeDtypeStruct(flow.shape, F32),
        ),
        in_specs=[pl.BlockSpec(memory_space=pltpu.HBM)] * 2,
        out_specs=(pl.BlockSpec(memory_space=pltpu.HBM),) * 2,
        scratch_shapes=[
            pltpu.VMEM((4, ROWS, 8, ny), F32),
            pltpu.VMEM((4, ROWS, ny), F32),
            pltpu.VMEM((4, 4, 2, ROWS, ny), F32),
            dma((10,)),
        ],
        compiler_params=pltpu.CompilerParams(vmem_limit_bytes=ALL_VMEM),
        name="place",
    )(blocks, flow_done)


def solution(mesh):
    placed = (
        P(("comp", "trc"), None, "space", None),
        P(("comp", "trc"), "space", None),
        P(),
        P("space", None),
        P("space", None),
    )
    return jax.shard_map(
        body,
        mesh=mesh,
        in_specs=placed,
        out_specs=(P(("comp", "trc"), None, "space", None), P(("comp", "trc"), "space", None)),
        check_vma=False,
    )
```

time: 134 us -> 81.1 us (0.61)
  Pallas kernels: 128 us -> 79.1 us
  local copies, waits for them, and re-layouts: 3.7 us -> 0 us
    pallas_call x1, Pallas kernels: 124 us -> 77 us  [body(): pl.pallas_call(kernel, out_shape=(jax.ShapeDtypeStruct((4, ROWS, 8, ny),...]
    unnamed x12 -> x0, local copies, waits for them, and re-layouts: 3.44 us -> none
    pallas_call x1, Pallas kernels: 3.51 us -> 2.11 us  [body(): pl.pallas_call(place, out_shape=(jax.ShapeDtypeStruct(tracers.shape, F32)...]
where the time goes in v1:
time: 81.1 us; the launch traced here: 79.9 us
  Pallas kernels  79.1 us (98%)
    pallas_call x1, Pallas kernels, body(): pl.pallas_call(kernel, out_shape=(jax.ShapeDtypeStruct((4, ROWS, 8, ny),...  77 us
    pallas_call x1, Pallas kernels, body(): pl.pallas_call(place, out_shape=(jax.ShapeDtypeStruct(tracers.shape, F32)...  2.11 us

profile of v1, /device:TPU:7, one launch (start us, length us, event | category | flops | bytes accessed | tf_op | source)
XLA Modules:
  0.0 79.9 jit_solution(18126792648677816607)
XLA Ops:
  0.6 77.0 %ocean.1 = (f32[4,8,8,1024]{3,2,1,0:T(8,128)}, f32[4,8,1024]{2,1,0:T(8,128)}) custom-call(f32[4,8,8,1024]{3,2,1,0:T(8,128)} %tracers.1, f32[4,8,1024]{2,1,0:T(8,128)} %flow.1, f32[16,16]{1,0:T(8,128)} %rates.1, s32[8,1024]{1,0:T(8,128)} %land.1, s32[8,1024]{1,0:T(8,128)} %layers.1), custom_call_target="tpu_custom_call" | custom-call | tf_op jit(solution)/shard_map/ocean/pallas_call | solution.py:693
  77.6 2.1 %place.1 = (f32[4,8,8,1024]{3,2,1,0:T(8,128)}, f32[4,8,1024]{2,1,0:T(8,128)}) custom-call(f32[4,8,8,1024]{3,2,1,0:T(8,128)} %get-tuple-element.4.blocks, f32[4,8,1024]{2,1,0:T(8,128)} %get-tuple-element.5.flow), custom_call_target="tpu_custom_call" | custom-call | tf_op jit(solution)/shard_map/place/pallas_call | solution.py:733

commit v2 on v1

--- a/solution.py
+++ b/solution.py
@@ -21,10 +21,12 @@
 DEEP = 24
 GHOST = 4
 SPAN = ROWS + 2 * GHOST
+EDGE = 128
 HALF = ROWS // 2
 ALL_VMEM = 67_043_328
 LINE = 8
-PAIR = 256
+PAIR = 128
+PAIRS = 2
 
 
 def limited(before, after):
@@ -73,6 +75,9 @@
         )
 
     middle = pl.ds(ROWS, ROWS)
+    mid = ny // 2
+    cut = mid + EDGE
+    width = mid + EDGE
 
     all_flow = pltpu.make_async_copy(flow, fl_v, fl_local.at[1])
     all_tr = pltpu.make_async_copy(tracers, tr_v, in_local.at[0])
@@ -215,41 +220,42 @@
     def _():
         dep_copy(1).start()
 
-    def halo_copy(step, slot, d):
+    def halo_copy(wave, slot, d):
         low = d < 0
-        return remote(
-            grid.at[step, slot, pl.ds(GHOST if low else ROWS, GHOST)],
-            grid.at[step, slot, pl.ds(GHOST + ROWS if low else 0, GHOST)],
-            halo_s.at[step, slot, 0 if low else 1], halo_r.at[step, slot, 1 if low else 0],
+        step, lanes = ((0, pl.ds(0, ny)), (1, pl.ds(0, cut)), (1, pl.ds(cut, ny - cut)))[wave]
+        return remote(
+            grid.at[step, slot, pl.ds(GHOST if low else ROWS, GHOST), :, lanes],
+            grid.at[step, slot, pl.ds(GHOST + ROWS if low else 0, GHOST), :, lanes],
+            halo_s.at[wave, slot, 0 if low else 1], halo_r.at[wave, slot, 1 if low else 0],
             holder(v, sp + d),
         )
 
-    def halo_start(step, slot):
+    def halo_start(wave, slot):
         @pl.when(has_prev)
         def _():
-            halo_copy(step, slot, -1).start()
+            halo_copy(wave, slot, -1).start()
 
         @pl.when(has_next)
         def _():
-            halo_copy(step, slot, 1).start()
-
-    def halo_wait(step, slot):
+            halo_copy(wave, slot, 1).start()
+
+    def halo_wait(wave, slot):
         @pl.when(has_prev)
         def _():
-            halo_copy(step, slot, 1).wait_recv()
+            halo_copy(wave, slot, 1).wait_recv()
 
         @pl.when(has_next)
         def _():
-            halo_copy(step, slot, -1).wait_recv()
-
-    def halo_sent(step, slot):
+            halo_copy(wave, slot, -1).wait_recv()
+
+    def halo_sent(wave, slot):
         @pl.when(has_prev)
         def _():
-            halo_copy(step, slot, -1).wait_send()
+            halo_copy(wave, slot, -1).wait_send()
 
         @pl.when(has_next)
         def _():
-            halo_copy(step, slot, 1).wait_send()
+            halo_copy(wave, slot, 1).wait_send()
 
     def regroup(slot):
         def tile(q, _):
@@ -308,9 +314,6 @@
 
     lane_deep = lax.broadcasted_iota(jnp.int32, (DEEP, ny), 1)
     top_half = lax.broadcasted_iota(jnp.int32, (8, ny), 0) < 4
-    lane = lax.broadcasted_iota(jnp.int32, (8, ny), 1)
-    at_first = lane == 0
-    at_last = lane == ny - 1
 
     def wet_of(level, rows):
         return jnp.where(depth_v[rows] > level.astype(F32), 1.0, 0.0)
@@ -359,23 +362,7 @@
                 coef_y[step, i - 2, k] = spread_rows(natural, 4 + k, i + shift)
         return 0
 
-    lax.fori_loop(0, STEPS, velocities, 0)
-
-    own_rows = slice(ROWS, 2 * ROWS)
-    above = jnp.where(v > 0, DIFFUSION, 0.0).astype(F32)
-    wet_a = wet_of(2 * v, own_rows)
-    wet_b = wet_of(2 * v + 1, own_rows)
-    natural[0, 0, 0:ROWS] = DIFFUSION * wet_a * wet_b
-    natural[1, 0, 0:ROWS] = DIFFUSION * wet_a * wet_b
-    natural[0, 1, 0:ROWS] = above * wet_a * wet_of(2 * v - 1, own_rows)
-    natural[1, 1, 0:ROWS] = DIFFUSION * wet_b * wet_of(2 * v + 2, own_rows)
-    for row in range(ROWS):
-        for k in range(2):
-            mix_w[row, k] = spread_rows(natural, k, row)
-
-    for comp in range(2):
-        for e in range(2):
-            velocity_send[comp, e] = field[STEPS, comp, e, own_rows]
+    velocities(0, 0)
 
     def velocity_copy(comp):
         return remote(
@@ -393,19 +380,37 @@
         velocity_send.at[c], flow_out.at[pl.ds(2 * c, 2)], fo_own.at[0]
     )
 
-    @pl.when(flip == 0)
-    def _():
-        velocity_own.start()
-        velocity_copy(1 - c).start()
-
-    @pl.when(flip == 1)
-    def _():
+    def later_velocities():
+        velocities(1, 0)
+        own_rows = slice(ROWS, 2 * ROWS)
+        above = jnp.where(v > 0, DIFFUSION, 0.0).astype(F32)
+        wet_a = wet_of(2 * v, own_rows)
+        wet_b = wet_of(2 * v + 1, own_rows)
+        natural[0, 0, 0:ROWS] = DIFFUSION * wet_a * wet_b
+        natural[1, 0, 0:ROWS] = DIFFUSION * wet_a * wet_b
+        natural[0, 1, 0:ROWS] = above * wet_a * wet_of(2 * v - 1, own_rows)
+        natural[1, 1, 0:ROWS] = DIFFUSION * wet_b * wet_of(2 * v + 2, own_rows)
+        for row in range(ROWS):
+            for k in range(2):
+                mix_w[row, k] = spread_rows(natural, k, row)
+
         for comp in range(2):
-            velocity_copy(comp).start()
-
-    def along_x(step, load, first_face, last_face, put):
+            for e in range(2):
+                velocity_send[comp, e] = field[STEPS, comp, e, own_rows]
+
+        @pl.when(flip == 0)
+        def _():
+            velocity_own.start()
+            velocity_copy(1 - c).start()
+
+        @pl.when(flip == 1)
+        def _():
+            for comp in range(2):
+                velocity_copy(comp).start()
+
+    def along_x(step, load, first_face, last_face, start, size, put):
         def chunk(q, _):
-            lanes = pl.ds(pl.multiple_of(q * PAIR, PAIR), PAIR)
+            lanes = pl.ds(pl.multiple_of(start + q * PAIR, 128), PAIR)
             before = load(first_face - 1, lanes)
             here = load(first_face, lanes)
             ahead = load(first_face + 1, lanes)
@@ -429,39 +434,53 @@
                 here, ahead, jump, slope = ahead, far, next_jump, next_slope
             return 0
 
-        lax.fori_loop(0, ny // PAIR, chunk, 0)
-
-    def along_y(step, i, a):
-        right = jnp.where(at_last, 0.0, roll_lanes(a, -1))
+        lax.fori_loop(0, size // PAIR, chunk, 0, unroll=PAIRS)
+
+    def along_y(step, i, a, lanes):
+        columns = lax.broadcasted_iota(jnp.int32, a.shape, 1)
+        right = jnp.where(columns == a.shape[1] - 1, 0.0, roll_lanes(a, -1))
         jump = right - a
-        slope = limited(jnp.where(at_first, a, roll_lanes(jump, 1)), jump)
+        slope = limited(jnp.where(columns == 0, a, roll_lanes(jump, 1)), jump)
         flux = (
-            coef_y[step, i - 2, 0] * a
-            + coef_y[step, i - 2, 1] * slope
-            + coef_y[step, i - 2, 2] * right
-            + coef_y[step, i - 2, 3] * roll_lanes(slope, -1)
-        )
-        return flux - roll_lanes(flux, 1)
-
-    def advance(step, slot):
-        def put_one(i, lanes, here, change):
-            part[i, :, lanes] = here + change
-
-        along_x(step, lambda i, lanes: grid[step, slot, i, :, lanes], 1, 13, put_one)
+            coef_y[step, i - 2, 0, :, lanes] * a
+            + coef_y[step, i - 2, 1, :, lanes] * slope
+            + coef_y[step, i - 2, 2, :, lanes] * right
+            + coef_y[step, i - 2, 3, :, lanes] * roll_lanes(slope, -1)
+        )
+        return flux - jnp.where(columns == 0, 0.0, roll_lanes(flux, 1))
+
+    def advance(step, slot, start, size, keep_start, keep_size):
+        lanes = pl.ds(start, size)
+        kept = pl.ds(keep_start, keep_size)
+        skip = keep_start - start
+
+        def put_one(i, at_lanes, here, change):
+            part[i, :, at_lanes] = here + change
+
+        along_x(
+            step, lambda i, at_lanes: grid[step, slot, i, :, at_lanes], 1, 13, start, size, put_one
+        )
 
         def row_one(i, _):
-            first[i] = part[i] + along_y(step, i, grid[step, slot, i])
+            first[i, :, lanes] = part[i, :, lanes] + along_y(
+                step, i, grid[step, slot, i, :, lanes], lanes
+            )
             return 0
 
         lax.fori_loop(2, 14, row_one, 0, unroll=True)
 
-        def put_two(i, lanes, here, change):
-            part[i, :, lanes] = (grid[step, slot, i, :, lanes] + here) + change
-
-        along_x(step, lambda i, lanes: first[i, :, lanes], 3, 11, put_two)
+        def put_two(i, at_lanes, here, change):
+            part[i, :, at_lanes] = (grid[step, slot, i, :, at_lanes] + here) + change
+
+        along_x(
+            step, lambda i, at_lanes: first[i, :, at_lanes], 3, 11, keep_start, keep_size, put_two
+        )
 
         def row_two(i, _):
-            second[slot, i - GHOST] = 0.5 * (part[i] + along_y(step, i, first[i]))
+            change = along_y(step, i, first[i, :, lanes], lanes)
+            second[slot, i - GHOST, :, kept] = 0.5 * (
+                part[i, :, kept] + change[:, skip : skip + keep_size]
+            )
             return 0
 
         lax.fori_loop(GHOST, GHOST + ROWS, row_two, 0, unroll=True)
@@ -469,56 +488,66 @@
     def swap_halves(a):
         return pltpu.roll(a, 4, 0)
 
-    def mix_copy(step, slot, d):
-        return remote(
-            packed.at[step, slot, 0 if d < 0 else 1], ext.at[step, 1 if d < 0 else 0, slot],
-            mix_s.at[step, slot, 0 if d < 0 else 1], mix_r.at[step, slot, 1 if d < 0 else 0],
+    kept_of = ((0, ny), (0, mid), (mid, ny - mid))
+
+    def mix_copy(wave, slot, d):
+        step, lanes = min(wave, 1), pl.ds(*kept_of[wave])
+        return remote(
+            packed.at[step, slot, 0 if d < 0 else 1, :, :, lanes],
+            ext.at[step, 1 if d < 0 else 0, slot, :, :, lanes],
+            mix_s.at[wave, slot, 0 if d < 0 else 1], mix_r.at[wave, slot, 1 if d < 0 else 0],
             holder(v + d, sp),
         )
 
-    def mix_start(step, slot):
+    def mix_start(wave, slot):
+        step, lanes = min(wave, 1), pl.ds(*kept_of[wave])
+        in_top = lax.broadcasted_iota(jnp.int32, (8, kept_of[wave][1]), 0) < 4
+
         def row(i, _):
-            a = second[slot, i]
-            b = second[slot, i + HALF]
-            packed[step, slot, 0, i] = jnp.where(top_half, a, swap_halves(b))
-            packed[step, slot, 1, i] = jnp.where(top_half, swap_halves(a), b)
+            a = second[slot, i, :, lanes]
+            b = second[slot, i + HALF, :, lanes]
+            packed[step, slot, 0, i, :, lanes] = jnp.where(in_top, a, swap_halves(b))
+            packed[step, slot, 1, i, :, lanes] = jnp.where(in_top, swap_halves(a), b)
             return 0
 
         lax.fori_loop(0, HALF, row, 0, unroll=True)
 
         @pl.when(v > 0)
         def _():
-            mix_copy(step, slot, -1).start()
+            mix_copy(wave, slot, -1).start()
 
         @pl.when(v < 3)
         def _():
-            mix_copy(step, slot, 1).start()
-
-    def mix_wait(step, slot):
+            mix_copy(wave, slot, 1).start()
+
+    def mix_wait(wave, slot):
         @pl.when(v > 0)
         def _():
-            mix_copy(step, slot, 1).wait_recv()
+            mix_copy(wave, slot, 1).wait_recv()
 
         @pl.when(v < 3)
         def _():
-            mix_copy(step, slot, -1).wait_recv()
-
-    def mix_sent(step, slot):
+            mix_copy(wave, slot, -1).wait_recv()
+
+    def mix_sent(wave, slot):
         @pl.when(v > 0)
         def _():
-            mix_copy(step, slot, -1).wait_send()
+            mix_copy(wave, slot, -1).wait_send()
 
         @pl.when(v < 3)
         def _():
-            mix_copy(step, slot, 1).wait_send()
-
-    def settle(step, put, start, stop):
+            mix_copy(wave, slot, 1).wait_send()
+
+    def settle(step, put, start, size):
+        lanes = pl.ds(start, size)
+        in_top = lax.broadcasted_iota(jnp.int32, (8, size), 0) < 4
+
         def reacted(i, beyond_of):
-            inner = mix_w[i, 0]
-            outer = mix_w[i, 1]
+            inner = mix_w[i, 0, :, lanes]
+            outer = mix_w[i, 1, :, lanes]
             mixed = []
             for slot in range(4):
-                a = second[slot, i]
+                a = second[slot, i, :, lanes]
                 beyond = beyond_of(slot)
                 mixed.append(a + inner * (swap_halves(a) - a) + outer * (beyond - a))
             whole = jnp.concatenate(mixed, axis=0)
@@ -527,89 +556,111 @@
                 matrix[...], soft, precision=lax.Precision.HIGHEST, preferred_element_type=F32
             )
             for slot in range(4):
-                put(slot, i, done[8 * slot : 8 * slot + 8])
+                put(slot, i, lanes, done[8 * slot : 8 * slot + 8])
 
         def rows(j, _):
             reacted(
                 j,
                 lambda slot: jnp.where(
-                    top_half, ext[step, 0, slot, j], swap_halves(ext[step, 1, slot, j])
+                    in_top,
+                    ext[step, 0, slot, j, :, lanes],
+                    swap_halves(ext[step, 1, slot, j, :, lanes]),
                 ),
             )
             reacted(
                 j + HALF,
                 lambda slot: jnp.where(
-                    top_half, swap_halves(ext[step, 0, slot, j]), ext[step, 1, slot, j]
+                    in_top,
+                    swap_halves(ext[step, 0, slot, j, :, lanes]),
+                    ext[step, 1, slot, j, :, lanes],
                 ),
             )
             return 0
 
-        lax.fori_loop(start, stop, rows, 0)
-
-    order = [w, 2 * (1 - c) + t, 2 * c + 1 - t, 2 * (1 - c) + 1 - t]
+        lax.fori_loop(0, HALF, rows, 0)
 
     between = jnp.logical_or(
         jnp.logical_and(has_prev, odd(sp - 1) != flip),
         jnp.logical_and(has_next, odd(sp + 1) != flip),
     )
-
-    def run(step):
-        if step == 0:
-
-            @pl.when(between)
-            def _():
-                for number in range(2):
-                    arrived(number)
-
-        for number, slot in enumerate(order):
-            halo_wait(step, slot)
-            advance(step, slot)
-            mix_start(step, slot)
-            if step == 0 and number < 2:
-
-                @pl.when(jnp.logical_not(between))
-                def _(number=number):
-                    arrived(number)
-        for slot in order:
-            mix_wait(step, slot)
-
-    run(0)
-
-    def put_next(slot, i, a):
-        grid[1, slot, GHOST + i] = a
-
-    settle(0, put_next, 0, HALF)
-    for slot in order:
-        halo_start(1, slot)
-    run(1)
-
-    def put_final(slot, i, a):
-        final[slot, i] = a
-
-    cuts = [(h, HALF * side + 2 * h) for h in range(2) for side in range(2)]
-
-    def out_copy(k, part_of, row):
+    near, far, last = 2 * (1 - c) + t, 2 * c + 1 - t, 2 * (1 - c) + 1 - t
+    order = [
+        w, jnp.where(between, far, near), jnp.where(between, last, far),
+        jnp.where(between, near, last),
+    ]
+
+    arrived(0)
+    for number, slot in enumerate(order):
+        if number == 2:
+            arrived(1)
+        if number == 3:
+            later_velocities()
+        halo_wait(0, slot)
+        advance(0, slot, 0, ny, 0, ny)
+        mix_start(0, slot)
+    for slot in range(4):
+        mix_wait(0, slot)
+
+    def put_next(slot, i, lanes, a):
+        grid[1, slot, GHOST + i, :, lanes] = a
+
+    for wave, (start, size) in ((1, (0, cut)), (2, (cut, ny - cut))):
+        settle(0, put_next, start, size)
+        for slot in range(4):
+            halo_start(wave, slot)
+
+    def put_final(slot, i, lanes, a):
+        final[slot, i, :, lanes] = a
+
+    def out_copy(k, wave):
         cc, tt = peers[k]
-        return remote(
-            final.at[2 * cc + tt, pl.ds(row, 2)], out.at[v, pl.ds(row, 2)],
-            out_s.at[k, part_of], out_r.at[v, part_of], at(cc, sp, tt),
-        )
-
-    def own_copy(part_of, row):
+        lanes = pl.ds(*kept_of[wave])
+        return remote(
+            final.at[2 * cc + tt, :, :, lanes], out.at[v, :, :, lanes],
+            out_s.at[k, wave], out_r.at[v, wave], at(cc, sp, tt),
+        )
+
+    def out_from(k, wave):
+        cc, tt = peers[k]
+        lanes = pl.ds(*kept_of[wave])
+        source = pair_of(cc, tt)
+        return remote(
+            final.at[w, :, :, lanes], out.at[source, :, :, lanes],
+            out_s.at[k, wave], out_r.at[source, wave], at(cc, sp, tt),
+        )
+
+    def own_copy(wave):
+        lanes = pl.ds(*kept_of[wave])
         return pltpu.make_async_copy(
-            final.at[w, pl.ds(row, 2)], out.at[v, pl.ds(row, 2)], own_out.at[part_of]
-        )
-
-    for h in range(2):
-        settle(1, put_final, 2 * h, 2 * h + 2)
-        for part_of, (when, row) in enumerate(cuts):
-            if when == h:
-                for k in range(3):
-                    out_copy(k, part_of, row).start()
-                own_copy(part_of, row).start()
-
-    for part_of, (_, row) in enumerate(cuts):
-        own_copy(part_of, row).wait()
+            final.at[w, :, :, lanes], out.at[v, :, :, lanes], own_out.at[wave]
+        )
+
+    def window(wave, slots):
+        def one(slot, _):
+            halo_wait(wave, slot)
+            start = (0, ny - width)[wave - 1]
+            advance(1, slot, start, width, *kept_of[wave])
+            mix_start(wave, slot)
+            return 0
+
+        lax.fori_loop(*slots, one, 0)
+
+    def finish(wave):
+        for slot in range(4):
+            mix_wait(wave, slot)
+        settle(1, put_final, *kept_of[wave])
+        for k in range(3):
+            out_copy(k, wave).start()
+        own_copy(wave).start()
+
+    window(1, (0, 4))
+    window(2, (0, 2))
+    finish(1)
+    window(2, (2, 4))
+    finish(2)
+
+    for wave in (1, 2):
+        own_copy(wave).wait()
 
     @pl.when(flip == 0)
     def _():
@@ -639,19 +690,14 @@
         dep_copy(1).wait_send()
         relay_copy(1).wait_send()
 
-    for step in range(STEPS):
+    for wave in range(3):
         for slot in range(4):
-            halo_sent(step, slot)
-            mix_sent(step, slot)
-    for k in range(3):
-        cc, tt = peers[k]
-        source = pair_of(cc, tt)
-        for part_of, (_, row) in enumerate(cuts):
-            out_copy(k, part_of, row).wait_send()
-            remote(
-                final.at[w, pl.ds(row, 2)], out.at[source, pl.ds(row, 2)],
-                out_s.at[k, part_of], out_r.at[source, part_of], at(cc, sp, tt),
-            ).wait_recv()
+            halo_sent(wave, slot)
+            mix_sent(wave, slot)
+    for wave in (1, 2):
+        for k in range(3):
+            out_copy(k, wave).wait_send()
+            out_from(k, wave).wait_recv()
 
 
 def place(blocks, flow, out, flow_out, held, held_flow, ready, sems):
@@ -720,9 +766,9 @@
             pltpu.VMEM((2, 2, ROWS, ny), F32),
             dma((3,)), dma((3, 2)), dma((4, 2)),
             dma((2,)), dma((2,)), dma((2,)), dma((3,)), dma((3,)), dma((3,)), dma((3,)),
-            dma((STEPS, 4, 2)), dma((STEPS, 4, 2)),
-            dma((STEPS, 4, 2)), dma((STEPS, 4, 2)),
-            dma((3, 4)), dma((4, 4)), dma((4,)),
+            dma((3, 4, 2)), dma((3, 4, 2)),
+            dma((3, 4, 2)), dma((3, 4, 2)),
+            dma((3, 3)), dma((4, 3)), dma((3,)),
             dma((2,)), dma((2,)), dma((1,)),
         ],
         compiler_params=pltpu.CompilerParams(

time: 81.1 us -> 81.7 us (level); the launches traced: 79.9 us -> 81.5 us
  Pallas kernels: 79.1 us -> 80.9 us
    pallas_call x1, Pallas kernels: 77 us -> 78.8 us  [body(): pl.pallas_call(kernel, out_shape=(jax.ShapeDtypeStruct((4, ROWS, 8, ny),...]
where the time goes in v2:
time: 81.7 us; the launch traced here: 81.5 us
  Pallas kernels  80.9 us (99%)
    pallas_call x1, Pallas kernels, body(): pl.pallas_call(kernel, out_shape=(jax.ShapeDtypeStruct((4, ROWS, 8, ny),...  78.8 us
    pallas_call x1, Pallas kernels, body(): pl.pallas_call(place, out_shape=(jax.ShapeDtypeStruct(tracers.shape, F32)...  2.11 us

profile of v2, /device:TPU:7, one launch (start us, length us, event | category | flops | bytes accessed | tf_op | source)
XLA Modules:
  0.0 81.5 jit_solution(3082057928032478025)
XLA Ops:
  0.6 78.8 %ocean.1 = (f32[4,8,8,1024]{3,2,1,0:T(8,128)}, f32[4,8,1024]{2,1,0:T(8,128)}) custom-call(f32[4,8,8,1024]{3,2,1,0:T(8,128)} %tracers.1, f32[4,8,1024]{2,1,0:T(8,128)} %flow.1, f32[16,16]{1,0:T(8,128)} %rates.1, s32[8,1024]{1,0:T(8,128)} %land.1, s32[8,1024]{1,0:T(8,128)} %layers.1), custom_call_target="tpu_custom_call" | custom-call | tf_op jit(solution)/shard_map/ocean/pallas_call | solution.py:739
  79.4 2.1 %place.1 = (f32[4,8,8,1024]{3,2,1,0:T(8,128)}, f32[4,8,1024]{2,1,0:T(8,128)}) custom-call(f32[4,8,8,1024]{3,2,1,0:T(8,128)} %get-tuple-element.4.blocks, f32[4,8,1024]{2,1,0:T(8,128)} %get-tuple-element.5.flow), custom_call_target="tpu_custom_call" | custom-call | tf_op jit(solution)/shard_map/place/pallas_call | solution.py:779

commit v3 on v2

--- a/solution.py
+++ b/solution.py
@@ -188,17 +188,19 @@
         for cc in range(2):
             flow_copy(cc).start()
 
-    def in_copy(k, e):
+    def in_copy(k, side, e):
         cc, tt = peers[k]
-        return remote(
-            tr_v.at[:, 2 * pair_of(cc, tt) + e], stage.at[w, e],
-            in_sem_s.at[k, e], in_sem_r.at[w, e], at(cc, sp, tt),
+        lanes = pl.ds(side * mid, mid)
+        return remote(
+            tr_v.at[:, 2 * pair_of(cc, tt) + e, :, lanes], stage.at[w, e, :, :, lanes],
+            in_sem_s.at[k, side, e], in_sem_r.at[w, side, e], at(cc, sp, tt),
         )
 
     all_tr.wait()
     for k in (2, 0, 1):
-        for e in range(2):
-            in_copy(k, e).start()
+        for side in range(2):
+            for e in range(2):
+                in_copy(k, side, e).start()
 
     def dep_copy(d):
         return remote(
@@ -222,7 +224,10 @@
 
     def halo_copy(wave, slot, d):
         low = d < 0
-        step, lanes = ((0, pl.ds(0, ny)), (1, pl.ds(0, cut)), (1, pl.ds(cut, ny - cut)))[wave]
+        step, lanes = (
+            (0, pl.ds(0, mid)), (1, pl.ds(0, cut)), (1, pl.ds(cut, ny - cut)),
+            (0, pl.ds(mid, ny - mid)),
+        )[wave]
         return remote(
             grid.at[step, slot, pl.ds(GHOST if low else ROWS, GHOST), :, lanes],
             grid.at[step, slot, pl.ds(GHOST + ROWS if low else 0, GHOST), :, lanes],
@@ -257,29 +262,33 @@
         def _():
             halo_copy(wave, slot, 1).wait_send()
 
-    def regroup(slot):
+    def regroup(slot, side):
         def tile(q, _):
             lanes = pl.ds(pl.multiple_of(q * 128, 128), 128)
             x = stage[slot, :, :, :, lanes].reshape(8, ROWS, 128)
             grid[0, slot, pl.ds(GHOST, ROWS), :, lanes] = jnp.swapaxes(x, 0, 1)
             return 0
 
-        lax.fori_loop(0, ny // 128, tile, 0, unroll=2)
+        tiles = mid // 128
+        lax.fori_loop(side * tiles, (side + 1) * tiles, tile, 0, unroll=2)
 
     def arrived(k):
         cc, tt = peers[k]
         slot = 2 * cc + tt
-        for e in range(2):
-            remote(
-                stage.at[slot, e], stage.at[slot, e], in_sem_s.at[k, e], in_sem_r.at[slot, e],
-                at(cc, sp, tt),
-            ).wait_recv()
-        regroup(slot)
-        halo_start(0, slot)
+        for side in range(2):
+            lanes = pl.ds(side * mid, mid)
+            for e in range(2):
+                remote(
+                    stage.at[slot, e, :, :, lanes], stage.at[slot, e, :, :, lanes],
+                    in_sem_s.at[k, side, e], in_sem_r.at[slot, side, e], at(cc, sp, tt),
+                ).wait_recv()
+            regroup(slot, side)
+            halo_start(3 * side, slot)
 
     for copy in own_tr:
         copy.wait()
-    regroup(w)
+    for side in range(2):
+        regroup(w, side)
 
     @pl.when(flip == 0)
     def _():
@@ -299,7 +308,8 @@
     def _():
         relay_copy(1).start()
 
-    halo_start(0, w)
+    for side in range(2):
+        halo_start(3 * side, w)
     arrived(2)
 
     @pl.when(has_prev)
@@ -585,17 +595,27 @@
     )
     near, far, last = 2 * (1 - c) + t, 2 * c + 1 - t, 2 * (1 - c) + 1 - t
     order = [
-        w, jnp.where(between, far, near), jnp.where(between, last, far),
+        jnp.where(between, far, w), jnp.where(between, last, near), jnp.where(between, w, far),
         jnp.where(between, near, last),
     ]
 
     arrived(0)
+
+    @pl.when(between)
+    def _():
+        arrived(1)
+
     for number, slot in enumerate(order):
         if number == 2:
-            arrived(1)
+
+            @pl.when(jnp.logical_not(between))
+            def _():
+                arrived(1)
+
         if number == 3:
             later_velocities()
         halo_wait(0, slot)
+        halo_wait(3, slot)
         advance(0, slot, 0, ny, 0, ny)
         mix_start(0, slot)
     for slot in range(4):
@@ -677,8 +697,9 @@
             flow_copy(cc).wait_send()
 
     for k in range(3):
-        for e in range(2):
-            in_copy(k, e).wait_send()
+        for side in range(2):
+            for e in range(2):
+                in_copy(k, side, e).wait_send()
 
     @pl.when(has_prev)
     def _():
@@ -690,9 +711,10 @@
         dep_copy(1).wait_send()
         relay_copy(1).wait_send()
 
-    for wave in range(3):
-        for slot in range(4):
+    for slot in range(4):
+        for wave in range(4):
             halo_sent(wave, slot)
+        for wave in range(3):
             mix_sent(wave, slot)
     for wave in (1, 2):
         for k in range(3):
@@ -764,9 +786,9 @@
             pltpu.VMEM((STEPS, 2, 4, HALF, 8, ny), F32),
             pltpu.VMEM((4, ROWS, 8, ny), F32),
             pltpu.VMEM((2, 2, ROWS, ny), F32),
-            dma((3,)), dma((3, 2)), dma((4, 2)),
+            dma((3,)), dma((3, 2, 2)), dma((4, 2, 2)),
             dma((2,)), dma((2,)), dma((2,)), dma((3,)), dma((3,)), dma((3,)), dma((3,)),
-            dma((3, 4, 2)), dma((3, 4, 2)),
+            dma((4, 4, 2)), dma((4, 4, 2)),
             dma((3, 4, 2)), dma((3, 4, 2)),
             dma((3, 3)), dma((4, 3)), dma((3,)),
             dma((2,)), dma((2,)), dma((1,)),

time: 81.7 us -> 79.3 us (0.971)
  Pallas kernels: 80.9 us -> 78.4 us
    pallas_call x1, Pallas kernels: 78.8 us -> 76.3 us  [body(): pl.pallas_call(kernel, out_shape=(jax.ShapeDtypeStruct((4, ROWS, 8, ny),...]
where the time goes in v3:
time: 79.3 us; the launch traced here: 79.1 us
  Pallas kernels  78.4 us (99%)
    pallas_call x1, Pallas kernels, body(): pl.pallas_call(kernel, out_shape=(jax.ShapeDtypeStruct((4, ROWS, 8, ny),...  76.3 us
    pallas_call x1, Pallas kernels, body(): pl.pallas_call(place, out_shape=(jax.ShapeDtypeStruct(tracers.shape, F32)...  2.11 us

profile of v3, /device:TPU:7, one launch (start us, length us, event | category | flops | bytes accessed | tf_op | source)
XLA Modules:
  0.0 79.1 jit_solution(15499467685102651090)
XLA Ops:
  0.6 76.3 %ocean.1 = (f32[4,8,8,1024]{3,2,1,0:T(8,128)}, f32[4,8,1024]{2,1,0:T(8,128)}) custom-call(f32[4,8,8,1024]{3,2,1,0:T(8,128)} %tracers.1, f32[4,8,1024]{2,1,0:T(8,128)} %flow.1, f32[16,16]{1,0:T(8,128)} %rates.1, s32[8,1024]{1,0:T(8,128)} %land.1, s32[8,1024]{1,0:T(8,128)} %layers.1), custom_call_target="tpu_custom_call" | custom-call | tf_op jit(solution)/shard_map/ocean/pallas_call | solution.py:761
  77.0 2.1 %place.1 = (f32[4,8,8,1024]{3,2,1,0:T(8,128)}, f32[4,8,1024]{2,1,0:T(8,128)}) custom-call(f32[4,8,8,1024]{3,2,1,0:T(8,128)} %get-tuple-element.4.blocks, f32[4,8,1024]{2,1,0:T(8,128)} %get-tuple-element.5.flow), custom_call_target="tpu_custom_call" | custom-call | tf_op jit(solution)/shard_map/place/pallas_call | solution.py:801

commit v4 on v3

--- a/solution.py
+++ b/solution.py
@@ -390,9 +390,9 @@
         velocity_send.at[c], flow_out.at[pl.ds(2 * c, 2)], fo_own.at[0]
     )
 
-    def later_velocities():
-        velocities(1, 0)
-        own_rows = slice(ROWS, 2 * ROWS)
+    own_rows = slice(ROWS, 2 * ROWS)
+
+    def mixing_weights():
         above = jnp.where(v > 0, DIFFUSION, 0.0).astype(F32)
         wet_a = wet_of(2 * v, own_rows)
         wet_b = wet_of(2 * v + 1, own_rows)
@@ -404,6 +404,8 @@
             for k in range(2):
                 mix_w[row, k] = spread_rows(natural, k, row)
 
+
+    def send_velocities():
         for comp in range(2):
             for e in range(2):
                 velocity_send[comp, e] = field[STEPS, comp, e, own_rows]
@@ -587,7 +589,7 @@
             )
             return 0
 
-        lax.fori_loop(0, HALF, rows, 0)
+        lax.fori_loop(0, HALF, rows, 0, unroll=2)
 
     between = jnp.logical_or(
         jnp.logical_and(has_prev, odd(sp - 1) != flip),
@@ -613,11 +615,12 @@
                 arrived(1)
 
         if number == 3:
-            later_velocities()
+            velocities(1, 0)
         halo_wait(0, slot)
         halo_wait(3, slot)
         advance(0, slot, 0, ny, 0, ny)
         mix_start(0, slot)
+    mixing_weights()
     for slot in range(4):
         mix_wait(0, slot)
 
@@ -628,6 +631,8 @@
         settle(0, put_next, start, size)
         for slot in range(4):
             halo_start(wave, slot)
+
+    send_velocities()
 
     def put_final(slot, i, lanes, a):
         final[slot, i, :, lanes] = a
@@ -674,9 +679,8 @@
         own_copy(wave).start()
 
     window(1, (0, 4))
-    window(2, (0, 2))
+    window(2, (0, 4))
     finish(1)
-    window(2, (2, 4))
     finish(2)
 
     for wave in (1, 2):

time: 79.3 us -> 75.5 us (0.952)
  Pallas kernels: 78.4 us -> 74.5 us
    pallas_call x1, Pallas kernels: 76.3 us -> 72.4 us  [body(): pl.pallas_call(kernel, out_shape=(jax.ShapeDtypeStruct((4, ROWS, 8, ny),...]
where the time goes in v4:
time: 75.5 us; the launch traced here: 75.2 us
  Pallas kernels  74.5 us (99%)
    pallas_call x1, Pallas kernels, body(): pl.pallas_call(kernel, out_shape=(jax.ShapeDtypeStruct((4, ROWS, 8, ny),...  72.4 us
    pallas_call x1, Pallas kernels, body(): pl.pallas_call(place, out_shape=(jax.ShapeDtypeStruct(tracers.shape, F32)...  2.11 us

profile of v4, /device:TPU:7, one launch (start us, length us, event | category | flops | bytes accessed | tf_op | source)
XLA Modules:
  0.0 75.2 jit_solution(6767144273842690941)
XLA Ops:
  0.6 72.4 %ocean.1 = (f32[4,8,8,1024]{3,2,1,0:T(8,128)}, f32[4,8,1024]{2,1,0:T(8,128)}) custom-call(f32[4,8,8,1024]{3,2,1,0:T(8,128)} %tracers.1, f32[4,8,1024]{2,1,0:T(8,128)} %flow.1, f32[16,16]{1,0:T(8,128)} %rates.1, s32[8,1024]{1,0:T(8,128)} %land.1, s32[8,1024]{1,0:T(8,128)} %layers.1), custom_call_target="tpu_custom_call" | custom-call | tf_op jit(solution)/shard_map/ocean/pallas_call | solution.py:765
  73.1 2.1 %place.1 = (f32[4,8,8,1024]{3,2,1,0:T(8,128)}, f32[4,8,1024]{2,1,0:T(8,128)}) custom-call(f32[4,8,8,1024]{3,2,1,0:T(8,128)} %get-tuple-element.4.blocks, f32[4,8,1024]{2,1,0:T(8,128)} %get-tuple-element.5.flow), custom_call_target="tpu_custom_call" | custom-call | tf_op jit(solution)/shard_map/place/pallas_call | solution.py:805

commit v5 on v4

--- a/solution.py
+++ b/solution.py
@@ -54,7 +54,7 @@
     has_next = sp < n - 1
 
     def odd(strip):
-        return lax.rem(strip // LINE, 2)
+        return lax.rem(strip // LINE + 1, 2)
 
     def flipped(bit, strip):
         return lax.rem(bit + odd(strip), 2)

time: 75.5 us -> 74.4 us (0.985)
  the two profiles are of different devices: /device:TPU:7 before, /device:TPU:38 now
where the time goes in v5:
time: 74.4 us; the launch traced here: 74.2 us
  Pallas kernels  73.6 us (99%)
    pallas_call x1, Pallas kernels, body(): pl.pallas_call(kernel, out_shape=(jax.ShapeDtypeStruct((4, ROWS, 8, ny),...  71.5 us
    pallas_call x1, Pallas kernels, body(): pl.pallas_call(place, out_shape=(jax.ShapeDtypeStruct(tracers.shape, F32)...  2.11 us

profile of v5, /device:TPU:38, one launch (start us, length us, event | category | flops | bytes accessed | tf_op | source)
XLA Modules:
  0.0 74.2 jit_solution(9927486640386941554)
XLA Ops:
  0.6 71.5 %ocean.1 = (f32[4,8,8,1024]{3,2,1,0:T(8,128)}, f32[4,8,1024]{2,1,0:T(8,128)}) custom-call(f32[4,8,8,1024]{3,2,1,0:T(8,128)} %tracers.1, f32[4,8,1024]{2,1,0:T(8,128)} %flow.1, f32[16,16]{1,0:T(8,128)} %rates.1, s32[8,1024]{1,0:T(8,128)} %land.1, s32[8,1024]{1,0:T(8,128)} %layers.1), custom_call_target="tpu_custom_call" | custom-call | tf_op jit(solution)/shard_map/ocean/pallas_call | solution.py:765
  72.1 2.1 %place.1 = (f32[4,8,8,1024]{3,2,1,0:T(8,128)}, f32[4,8,1024]{2,1,0:T(8,128)}) custom-call(f32[4,8,8,1024]{3,2,1,0:T(8,128)} %get-tuple-element.4.blocks, f32[4,8,1024]{2,1,0:T(8,128)} %get-tuple-element.5.flow), custom_call_target="tpu_custom_call" | custom-call | tf_op jit(solution)/shard_map/place/pallas_call | solution.py:805
